TPU v7x, 32 devices: a whole 2x2x4 slice. The times are simulated.
32 devices in a mesh: ep: 8 (over z, x), rep: 4 (over y, core).
Axes of the slice: x: 2, y: 2, z: 4, core: 2. Of those that a mesh axis runs over, the one named last changes fastest.
Arguments:
- tension: float32 [4096, 512], P(('rep', 'ep')), parts along dimension 0, may hold values from -6 to 6
- tile_dest: int32 [4096], P(('rep', 'ep')), parts along dimension 0, may hold values from 0 to 1023, as said below
- restriction: float32 [8, 64], replicated, may hold values from -0.75 to 0.75
- elem_block: int32 [32768], P(('rep', 'ep')), parts along dimension 0, may hold values from 0 to 1023
- shared_own: int32 [8192], P(('rep', 'ep')), parts along dimension 0, may hold values from 0 to 1023, as said below
- shared_send: int32 [8192], P(('rep', 'ep')), parts along dimension 0, may hold values from 0 to 1023
Outputs:
- quadrature: float32 [8, 32768], P(None, ('rep', 'ep')), parts along dimension 1
There are 4 independent parts, one for each index of `rep`. A program takes and returns all parts, laid end to end along the dimension named above; an argument that names none is the same for every part. Nothing has to cross between parts.
Inputs may be any that keep to these rules, and one draw needn't show every extreme that they name: `tile_dest`: A permutation of the tile positions. The 128 entries of one device name, for each device's block of 128 positions, either exactly 32 positions in it or none. `shared_own`: the 256 entries of one device are distinct.
All inputs are finite; a program needn't handle non-finite values.
Results may differ from a plain program's by a relative error of at most 0.00007.
Values sent between devices are 32-bit elements; how exact they have to be, the bound alone decides.
A program may use at most 64 MiB of HBM per device.

v0:
```python
import jax
import jax.numpy as jnp
from jax import lax
from jax.sharding import PartitionSpec as P

ELEM_NODES = 64


def from_behind(array, axis, by):
    length = lax.axis_size(axis)
    return lax.ppermute(array, axis, [(i, (i + by) % length) for i in range(length)])


def per_device(tension, tile_dest, restriction, elem_block, shared_own, shared_send):
    tile_dev = tension.shape[0]
    peer_count = lax.axis_size("ep")
    capacity = 2 * tile_dev // peer_count
    target = tile_dest // tile_dev
    onehot = (target[:, None] == jnp.arange(peer_count, dtype=jnp.int32)[None, :]).astype(jnp.int32)
    before = jnp.cumsum(onehot, axis=0) - onehot
    send_rank = jnp.sum(before * onehot, axis=1)
    send_slot = target * capacity + send_rank
    where_to = (
        jnp.full((peer_count * capacity,), tile_dev, jnp.int32)
        .at[send_slot]
        .set(tile_dest % tile_dev)
    )
    where_to = where_to.reshape(peer_count, capacity)
    local_quad = jnp.dot(
        tension.reshape(-1, ELEM_NODES),
        restriction.T,
        precision=lax.Precision.HIGHEST,
        preferred_element_type=jnp.float32,
    )
    local_quad = local_quad.reshape(tile_dev, -1)
    row_width = local_quad.shape[1]
    outbox = (
        jnp.zeros((peer_count * capacity, row_width), jnp.float32).at[send_slot].set(local_quad)
    )
    inbox, arrivals = (
        lax.all_to_all(
            outbox.reshape(peer_count, capacity, row_width),
            "ep",
            split_axis=0,
            concat_axis=0,
            tiled=True,
        ),
        lax.all_to_all(where_to, "ep", split_axis=0, concat_axis=0, tiled=True),
    )
    placed = (
        jnp.zeros((tile_dev, row_width), jnp.float32)
        .at[arrivals.reshape(-1)]
        .set(inbox.reshape(peer_count * capacity, row_width), mode="drop")
    )
    quad_values = placed.reshape(-1, restriction.shape[0])[elem_block]
    outgoing = quad_values[shared_send]
    incoming = from_behind(outgoing, "ep", -1)
    mixed = 0.5 * (quad_values[shared_own] + incoming)
    averaged = quad_values.at[shared_own].set(mixed)
    return averaged.T


def solution(mesh):
    return jax.shard_map(
        per_device,
        mesh=mesh,
        in_specs=(
            P(("rep", "ep"), None),
            P(("rep", "ep")),
            P(),
            P(("rep", "ep")),
            P(("rep", "ep")),
            P(("rep", "ep")),
        ),
        out_specs=P(None, ("rep", "ep")),
        check_vma=False,
    )
```

profile of v0, /device:TPU:0, one launch (start us, length us, event | category | flops | bytes accessed | tf_op | source)
XLA Modules:
  0.0 41.1 jit_solution(2360985464015724369)
XLA Ops:
  0.0 0.0 copy-start
  0.0 0.7 %and_select_fusion = (s32[128]{0:T(128)S(1)}, s32[128]{0:T(128)S(1)}) fusion(s32[128]{0:T(128)} %param.7), kind=kLoop, calls=%fused_computation.26 | loop fusion | flops 2432 | bytes 1536 | tf_op jit(solution)/shard_map/jit(remainder)/select_n | solution.py:26
  0.7 0.1 fusion.6
  0.8 0.2 reduce_window_sum.11
  1.0 0.2 select_reduce_fusion
  1.2 1.0 %scatter_custom_fusion = s32[256]{0:T(256)S(1)} fusion(s32[128]{0:T(128)S(1)} %compare_select_fusion.4, s32[128]{0:T(128)S(1)} %get-tuple-element.5, s32[]{:T(128)} %constant.39.clone.1), kind=kCustom, calls=%fused_computation.31 | custom fusion | bytes 1028 | tf_op jit(solution)/shard_map/scatter | solution.py:26
  2.2 0.7 %all_to_all.9 = s32[8,1,32]{2,1,0:T(1,128)} reshape(s32[256]{0:T(256)S(1)} %scatter_custom_fusion) | data formatting | bytes 2048 | tf_op jit(solution)/shard_map/all_to_all | solution.py:48
  2.8 7.4 %all-to-all-start = ((s32[8,1,32]{2,1,0:T(1,128)}), s32[8,1,32]{2,1,0:T(1,128)S(1)}, u32[]{:S(2)}, u32[]{:S(2)}) async-start(s32[8,1,32]{2,1,0:T(1,128)} %all_to_all.9), calls=%async_computation | async-start | bytes 8192 | tf_op jit(solution)/shard_map/all_to_all | solution.py:48
  10.3 0.0 copy-start.4
  10.3 0.7 %copy-done.4 = s32[256]{0:T(256)S(1)} copy-done((s32[256]{0:T(256)S(1)}, s32[256]{0:T(256)}, u32[]{:S(2)}) %copy-start.4) | copy-done | bytes 1048
  11.0 0.1 reshape.53
  11.1 0.5 %fusion.13 = f32[1024,8]{1,0:T(8,128)S(1)} fusion(f32[1024,64]{1,0:T(8,128)S(1)} %reshape.53, f32[8,64]{1,0:T(8,128)S(1)} %copy-done), kind=kOutput, calls=%fused_computation.34 | convolution fusion | flops 6291456 | bytes 296960 | tf_op jit(solution)/shard_map/dot_general | solution.py:29
  11.7 0.2 reshape.94
  11.9 0.9 %scatter_custom_fusion.1 = f32[256,64]{1,0:T(8,128)S(1)} fusion(s32[128]{0:T(128)S(1)} %compare_select_fusion.4, f32[128,64]{1,0:T(8,128)S(1)} %reshape.94, f32[]{:T(128)} %constant.38.clone.1), kind=kCustom, calls=%fused_computation.11 | custom fusion | bytes 65540 | tf_op jit(solution)/shard_map/scatter | solution.py:38
  12.8 0.7 %reshape.145 = f32[8,1,2048]{2,1,0:T(1,128)} reshape(f32[8,32,64]{2,1,0:T(8,128)S(1)} %bitcast.11) | data formatting | bytes 131072
  13.5 3.1 %all-to-all-done = s32[8,1,32]{2,1,0:T(1,128)S(1)} async-done(((s32[8,1,32]{2,1,0:T(1,128)}), s32[8,1,32]{2,1,0:T(1,128)S(1)}, u32[]{:S(2)}, u32[]{:S(2)}) %all-to-all-start) | async-done | bytes 1056 | tf_op jit(solution)/shard_map/all_to_all | solution.py:48
  16.7 3.3 %all-to-all-start.1 = ((f32[8,1,2048]{2,1,0:T(1,128)}), f32[8,1,2048]{2,1,0:T(1,128)S(1)}, u32[]{:S(2)}, u32[]{:S(2)}) async-start(f32[8,1,2048]{2,1,0:T(1,128)} %reshape.145), calls=%async_computation.1 | async-start | bytes 131072 | tf_op jit(solution)/shard_map/all_to_all | solution.py:41
  20.0 0.5 %broadcast.92 = s32[]{:T(128)} broadcast(s32[]{:T(128)} %constant.41.clone.1), dimensions={} | broadcast | bytes 8 | tf_op jit(solution)/shard_map/all_to_all | solution.py:48
  20.5 0.7 %reduce.3 = s32[8,32]{1,0:T(8,128)S(1)} reduce(s32[8,1,32]{2,1,0:T(1,128)S(1)} %all-to-all-done, s32[]{:T(128)} %broadcast.92), dimensions={1}, to_apply=%all_to_all.10.reduce_sub_computation.3 | reduce | bytes 2052 | tf_op jit(solution)/shard_map/all_to_all | solution.py:48
  21.2 0.1 reshape.52
  21.3 5.6 %all-to-all-done.1 = f32[8,1,2048]{2,1,0:T(1,128)S(1)} async-done(((f32[8,1,2048]{2,1,0:T(1,128)}), f32[8,1,2048]{2,1,0:T(1,128)S(1)}, u32[]{:S(2)}, u32[]{:S(2)}) %all-to-all-start.1) | async-done | bytes 65568 | tf_op jit(solution)/shard_map/all_to_all | solution.py:41
  26.9 0.5 %broadcast.93 = f32[]{:T(128)} broadcast(f32[]{:T(128)} %constant.82), dimensions={} | broadcast | bytes 8 | tf_op jit(solution)/shard_map/all_to_all | solution.py:41
  27.4 0.8 %reduce.4 = f32[8,2048]{1,0:T(8,128)S(1)} reduce(f32[8,1,2048]{2,1,0:T(1,128)S(1)} %all-to-all-done.1, f32[]{:T(128)} %broadcast.93), dimensions={1}, to_apply=%all_to_all.11.reduce_sub_computation | reduce | bytes 131076 | tf_op jit(solution)/shard_map/all_to_all | solution.py:41
  28.2 0.1 reshape.146
  28.3 1.2 %scatter_custom_fusion.2 = f32[128,64]{1,0:T(8,128)S(1)} fusion(s32[256]{0:T(256)S(1)} %bitcast.13, f32[256,64]{1,0:T(8,128)S(1)} %bitcast.12, f32[]{:T(128)} %constant.38.clone.1), kind=kCustom, calls=%fused_computation.16 | custom fusion | bytes 32772 | tf_op jit(solution)/shard_map/scatter | solution.py:53
  29.4 0.2 reshape.57
  29.6 2.8 %gather_fusion = f32[1024,8]{1,0:T(8,128)S(1)} fusion(f32[1024,8]{1,0:T(8,128)S(1)} %reshape.57, s32[1024]{0:T(1024)S(1)} %fusion.9), kind=kCustom, calls=%fused_computation | custom fusion | bytes 69632 | tf_op jit(solution)/shard_map/gather | solution.py:55
  32.5 0.7 %gather_fusion.1 = f32[256,8]{1,0:T(8,128)S(1)} fusion(f32[1024,8]{1,0:T(8,128)S(1)} %gather_fusion, s32[1024]{0:T(1024)S(1)} %pad_clamp_fusion), kind=kCustom, calls=%fused_computation.2 | custom fusion | bytes 17408 | tf_op jit(solution)/shard_map/gather | solution.py:56
  33.2 0.8 %collective-permute-start = (f32[256,8]{1,0:T(8,128)S(1)}, f32[256,8]{1,0:T(8,128)S(1)}, u32[]{:S(2)}, u32[]{:S(2)}) collective-permute-start(f32[256,8]{1,0:T(8,128)S(1)} %gather_fusion.1), channel_id=1, source_target_pairs={{0,28},{4,0},{8,4},{12,8},{16,12},{20,16},{24,20},{28,24},{1,29},{... | collective-permute-start | bytes 24584 | tf_op jit(solution)/shard_map/ppermute | solution.py:11
  34.0 4.2 %collective-permute-done = f32[256,8]{1,0:T(8,128)S(1)} collective-permute-done((f32[256,8]{1,0:T(8,128)S(1)}, f32[256,8]{1,0:T(8,128)S(1)}, u32[]{:S(2)}, u32[]{:S(2)}) %collective-permute-start) | collective-permute-done | bytes 8224 | tf_op jit(solution)/shard_map/ppermute | solution.py:11
  38.2 2.1 %scatter_custom_fusion.3 = f32[1024,8]{1,0:T(8,128)S(1)} fusion(f32[1024,8]{1,0:T(8,128)S(1)} %gather_fusion, s32[256]{0:T(256)S(1)} %compare_select_fusion.3, f32[256,8]{1,0:T(8,128)S(1)} %collective-permute-done, f32[]{:T(128)} %constant.48.clone.1, s32[1024]{0:T(1024)S(1)} %pad_clamp_fusion.1), kind=kCustom, calls=%fused_computation.7 | custom fusion | flops 4096 | bytes 692228 | tf_op jit(solution)/shard_map/scatter | solution.py:59
  40.3 0.8 %copy.9 = f32[8,1024]{1,0:T(8,128)} copy(f32[8,1024]{0,1:T(8,128)S(1)} %bitcast.10) | data formatting | bytes 65536 | tf_op jit(solution)/shard_map/transpose | solution.py:60
  (14 shorter events, 0.1 us)
Async XLA Ops:
  0.0 11.1 %copy-start = (f32[8,64]{1,0:T(8,128)S(1)}, f32[8,64]{1,0:T(8,128)}, u32[]{:S(2)}) copy-start(f32[8,64]{1,0:T(8,128)} %param.8) | copy-start | bytes 6148
  0.0 10.9 %copy-start.1 = (f32[128,512]{1,0:T(8,128)S(1)}, f32[128,512]{1,0:T(8,128)}, u32[]{:S(2)}) copy-start(f32[128,512]{1,0:T(8,128)} %param.6) | copy-start | bytes 786436
  2.8 7.4 %copy-start.3 = (s32[256]{0:T(256)S(1)}, s32[256]{0:T(256)}, u32[]{:S(2)}) copy-start(s32[256]{0:T(256)} %param.10) | copy-start | bytes 3076
  2.8 8.1 %copy-start.2 = (s32[1024]{0:T(1024)S(1)}, s32[1024]{0:T(1024)}, u32[]{:S(2)}) copy-start(s32[1024]{0:T(1024)} %param.9) | copy-start | bytes 12292
  2.8 13.8 %all-to-all-start = ((s32[8,1,32]{2,1,0:T(1,128)}), s32[8,1,32]{2,1,0:T(1,128)S(1)}, u32[]{:S(2)}, u32[]{:S(2)}) async-start(s32[8,1,32]{2,1,0:T(1,128)} %all_to_all.9), calls=%async_computation | async-start | bytes 8192 | tf_op jit(solution)/shard_map/all_to_all | solution.py:48
  10.3 0.7 %copy-start.4 = (s32[256]{0:T(256)S(1)}, s32[256]{0:T(256)}, u32[]{:S(2)}) copy-start(s32[256]{0:T(256)} %param.11) | copy-start | bytes 3076
  16.7 10.2 %all-to-all-start.1 = ((f32[8,1,2048]{2,1,0:T(1,128)}), f32[8,1,2048]{2,1,0:T(1,128)S(1)}, u32[]{:S(2)}, u32[]{:S(2)}) async-start(f32[8,1,2048]{2,1,0:T(1,128)} %reshape.145), calls=%async_computation.1 | async-start | bytes 131072 | tf_op jit(solution)/shard_map/all_to_all | solution.py:41
  33.2 5.0 %collective-permute-start = (f32[256,8]{1,0:T(8,128)S(1)}, f32[256,8]{1,0:T(8,128)S(1)}, u32[]{:S(2)}, u32[]{:S(2)}) collective-permute-start(f32[256,8]{1,0:T(8,128)S(1)} %gather_fusion.1), channel_id=1, source_target_pairs={{0,28},{4,0},{8,4},{12,8},{16,12},{20,16},{24,20},{28,24},{1,29},{... | collective-permute-start | bytes 24584 | tf_op jit(solution)/shard_map/ppermute | solution.py:11
where the time goes:
time: 41.4 us; the launch traced here: 41.1 us
  waiting for transfers between devices  12.9 us (31%)
  starting transfers between devices  11.6 us (28%)
  local copies, waits for them, and re-layouts  11.2 us (27%)
  other arithmetic  4.76 us (11%)
  matrix products  0.55 us (1%)
    all_to_all x1, starting transfers between devices, per_device(): lax.all_to_all(where_to, 'ep', split_axis=0, concat_axis=0, tiled=True)  7.41 us
    all_to_all x1, waiting for transfers between devices, per_device(): lax.all_to_all(outbox.reshape(peer_count, capacity, row_width), 'ep', spl...  5.58 us
    ppermute x1, waiting for transfers between devices, from_behind(): lax.ppermute(array, axis, [(i, (i + by) % length) for i in range(length)])  4.18 us
    all_to_all x1, starting transfers between devices, per_device(): lax.all_to_all(outbox.reshape(peer_count, capacity, row_width), 'ep', spl...  3.35 us
    all_to_all x1, waiting for transfers between devices, per_device(): lax.all_to_all(where_to, 'ep', split_axis=0, concat_axis=0, tiled=True)  3.13 us
    gather x1, local copies, waits for them, and re-layouts, per_device(): quad_values = placed.reshape(-1, restriction.shape[0])[elem_block]  2.81 us
    scatter x1, other arithmetic, per_device(): averaged = quad_values.at[shared_own].set(mixed)  2.12 us
    unnamed x12, local copies, waits for them, and re-layouts  1.51 us
  transfers between devices with their start and end apart: 3, of which 3 were waited for; matrix products, arithmetic and copies ran while one was open for 9% of the time, Pallas kernels for 0%

commit v1 on v0

v1 whole, which is shorter than its diff:
```python
import functools

import jax
import jax.numpy as jnp
from jax import lax
from jax.experimental import pallas as pl
from jax.experimental.pallas import tpu as pltpu
from jax.sharding import PartitionSpec as P

F32 = jnp.float32
BF16 = jnp.bfloat16
I32 = jnp.int32
MINOR = (((1,), (1,)), ((), ()))


def iota(shape, dim):
    return lax.broadcasted_iota(I32, shape, dim)


def pieces(x):
    high = x.astype(BF16)
    rest = x - high.astype(F32)
    mid = rest.astype(BF16)
    low = (rest - mid.astype(F32)).astype(BF16)
    return jnp.concatenate([high, mid, low], axis=1)


def select_rows(onehot, x):
    lanes = x.shape[1]
    got = jnp.dot(onehot, pieces(x), preferred_element_type=F32)
    return got[:, :lanes] + got[:, lanes : 2 * lanes] + got[:, 2 * lanes :]


def lanes_of(x, index):
    return jnp.take_along_axis(x, index, axis=1, mode="promise_in_bounds")


def kernel(
    n, cap, tension, dest, restriction, block, own, send, out,
    outbox, inbox, ghost_out, ghost_in, send_sem, recv_sem, ghost_sem,
):
    me = lax.axis_index("ep")
    tiles = tension.shape[0]
    quad, nodes = restriction.shape
    width = tension.shape[1] // nodes * quad
    lanes = 2 * width
    rows_e = block.shape[0]
    halves = own.shape[0]
    wide = tiles * halves

    barrier = pltpu.get_barrier_semaphore()
    for k in range(1, n):
        pl.semaphore_signal(barrier, inc=1, device_id={"ep": lax.rem(me + k, n)})

    for h in range(halves):
        want = jnp.broadcast_to(send[h : h + 1, :], (rows_e, tiles))
        got = lanes_of(block[...], lax.rem(want, tiles))
        ghost_out[h : h + 1, :] = jnp.sum(
            jnp.where(lax.div(want, tiles) == iota((rows_e, tiles), 0), got, 0),
            axis=0, keepdims=True,
        )

    place = dest[...]
    target = lax.div(place, tiles)
    to_peer = jnp.broadcast_to(target, (n, tiles)) == iota((n, tiles), 0)
    to_peer = to_peer.astype(F32)
    earlier = (iota((tiles, tiles), 0) < iota((tiles, tiles), 1)).astype(F32).astype(BF16)
    before = jnp.dot(to_peer.astype(BF16), earlier, preferred_element_type=F32)
    rank = jnp.sum(before * to_peer, axis=0, keepdims=True).astype(I32)
    slot = target * cap + rank
    slots = n * cap
    pack = (jnp.broadcast_to(slot, (slots, tiles)) == iota((slots, tiles), 0)).astype(F32).astype(BF16)
    at_rank = jnp.broadcast_to(rank, (tiles, tiles)) == lax.rem(iota((tiles, tiles), 0), cap)
    where_to = (to_peer * (lax.rem(place, tiles) + 1).astype(F32)).astype(BF16)
    where_to = lax.dot_general(
        where_to, at_rank.astype(F32).astype(BF16), MINOR, preferred_element_type=F32
    )

    full = (lanes, tension.shape[1])
    weight = jnp.concatenate([restriction[...]] * (full[1] // nodes), axis=1)
    weight = jnp.concatenate([weight] * (lanes // quad), axis=0)
    mine = lax.div(lax.rem(iota(full, 0), width), quad) == lax.div(iota(full, 1), nodes)
    weight = jnp.where(mine, weight, 0.0)
    local = lax.dot_general(
        tension[...], weight, MINOR,
        precision=lax.Precision.HIGHEST, preferred_element_type=F32,
    )
    packed = select_rows(pack, local)
    first = iota((cap, lanes), 1) < width
    for p in range(n):
        after = (p + 1) % n
        outbox[p, :cap, :] = jnp.where(
            first, packed[p * cap : (p + 1) * cap], packed[after * cap : (after + 1) * cap]
        )
        outbox[p, cap : cap + 1, :] = where_to[p : p + 1]
        outbox[p, cap + 1 : cap + 2, :] = where_to[after : after + 1]

    pl.semaphore_wait(barrier, n - 1)
    copies = []
    for k in range(1, n):
        peer = lax.rem(me + k, n)
        copies.append(
            pltpu.make_async_remote_copy(
                src_ref=outbox.at[peer],
                dst_ref=inbox.at[me],
                send_sem=send_sem.at[k],
                recv_sem=recv_sem.at[k],
                device_id={"ep": peer},
            )
        )
    ghosts = pltpu.make_async_remote_copy(
        src_ref=ghost_out,
        dst_ref=ghost_in,
        send_sem=ghost_sem.at[0],
        recv_sem=ghost_sem.at[1],
        device_id={"ep": lax.rem(me + n - 1, n)},
    )
    ghosts.start()
    for copy in copies:
        copy.start()
    inbox[me] = outbox[me]

    owned = jnp.concatenate([own[h : h + 1, :] for h in range(halves)], axis=1)
    entry = (iota((rows_e, wide), 1) + 1).astype(F32)
    entry = jnp.where(
        jnp.broadcast_to(lax.div(owned, tiles), (rows_e, wide)) == iota((rows_e, wide), 0), entry, 0.0
    ).astype(BF16)
    column = jnp.broadcast_to(lax.rem(owned, tiles), (tiles, wide)) == iota((tiles, wide), 0)
    shared = lax.dot_general(
        entry, column.astype(F32).astype(BF16), MINOR, preferred_element_type=F32
    ).astype(I32)

    ghosts.wait()
    for copy in copies:
        copy.wait()

    per = tiles // cap
    lane = lax.div(iota((1, tiles), 1), cap)
    onehot = []
    for which in range(2):
        parts = []
        for h in range(slots // tiles):
            pos = jnp.zeros((1, tiles), F32)
            for s in range(per):
                pos = jnp.where(lane == s, inbox[h * per + s, cap + which : cap + which + 1, :], pos)
            pos = jnp.broadcast_to(pos.astype(I32), (tiles, tiles))
            parts.append((pos == iota((tiles, tiles), 0) + 1).astype(F32).astype(BF16))
        onehot.append(jnp.concatenate(parts, axis=1))
    arrived = jnp.concatenate([inbox[s, :cap, :] for s in range(n)], axis=0)
    placed = select_rows(jnp.concatenate(onehot, axis=0), arrived)
    placed = jnp.where(iota((tiles, lanes), 1) < width, placed[:tiles], placed[tiles:]).T

    def values(index, base):
        index = jnp.broadcast_to(index, (quad, tiles))
        blocks = width // quad
        tile, part = lax.div(index, blocks), lax.rem(index, blocks)
        got = lanes_of(placed[base : base + quad], tile)
        for b in range(1, blocks):
            low = base + b * quad
            got = jnp.where(part == b, lanes_of(placed[low : low + quad], tile), got)
        return got

    ghost = [values(ghost_in[h : h + 1, :], width) for h in range(halves)]
    for r in range(rows_e):
        mine = values(block[r : r + 1, :], 0)
        which = jnp.broadcast_to(shared[r : r + 1, :], (quad, tiles))
        number = jnp.maximum(which - 1, 0)
        other = lanes_of(ghost[0], lax.rem(number, tiles))
        for h in range(1, halves):
            other = jnp.where(
                lax.div(number, tiles) == h, lanes_of(ghost[h], lax.rem(number, tiles)), other
            )
        out[:, r * tiles : (r + 1) * tiles] = jnp.where(which > 0, 0.5 * (mine + other), mine)


def per_device(tension, tile_dest, restriction, elem_block, shared_own, shared_send):
    n = lax.axis_size("ep")
    tiles = tension.shape[0]
    cap = 2 * tiles // n
    quad, nodes = restriction.shape
    lanes = 2 * (tension.shape[1] // nodes * quad)
    halves = shared_own.shape[0] // tiles
    vmem = pl.BlockSpec(memory_space=pltpu.VMEM)
    return pl.pallas_call(
        functools.partial(kernel, n, cap),
        out_shape=jax.ShapeDtypeStruct((quad, elem_block.shape[0]), F32),
        in_specs=[vmem] * 6,
        out_specs=vmem,
        scratch_shapes=[
            pltpu.VMEM((n, cap + 2, lanes), F32),
            pltpu.VMEM((n, cap + 2, lanes), F32),
            pltpu.VMEM((halves, tiles), I32),
            pltpu.VMEM((halves, tiles), I32),
            pltpu.SemaphoreType.DMA((n,)),
            pltpu.SemaphoreType.DMA((n,)),
            pltpu.SemaphoreType.DMA((2,)),
        ],
        compiler_params=pltpu.CompilerParams(collective_id=0, has_side_effects=True),
    )(
        tension,
        tile_dest.reshape(1, tiles),
        restriction,
        elem_block.reshape(-1, tiles),
        shared_own.reshape(halves, tiles),
        shared_send.reshape(halves, tiles),
    )


def solution(mesh):
    return jax.shard_map(
        per_device,
        mesh=mesh,
        in_specs=(
            P(("rep", "ep"), None),
            P(("rep", "ep")),
            P(),
            P(("rep", "ep")),
            P(("rep", "ep")),
            P(("rep", "ep")),
        ),
        out_specs=P(None, ("rep", "ep")),
        check_vma=False,
    )
```

time: 41.4 us -> 13.4 us (0.32)
  waiting for transfers between devices: 12.9 us -> 0 us
  Pallas kernels: 0 us -> 11.9 us
  starting transfers between devices: 11.6 us -> 0 us
  local copies, waits for them, and re-layouts: 11.2 us -> 1.38 us
  other arithmetic: 4.76 us -> 0 us
  matrix products: 0.55 us -> 0 us
    pallas_call x0 -> x1, Pallas kernels: none -> 11.9 us  [per_device(): pl.pallas_call(functools.partial(kernel, n, cap), out_shape=jax.ShapeDtyp...]
    all_to_all x2 -> x0, starting transfers between devices: 10.8 us -> none  [the longest x1 7.41 us: per_device(): lax.all_to_all(where_to, 'ep', split_axis=0, concat_axis=0, tiled=True)]
    all_to_all x2 -> x0, waiting for transfers between devices: 8.71 us -> none  [the longest x1 5.58 us: per_device(): lax.all_to_all(outbox.reshape(peer_count, capacity, row_width), 'ep', spl...]
    ppermute x1 -> x0, waiting for transfers between devices: 4.18 us -> none  [from_behind(): lax.ppermute(array, axis, [(i, (i + by) % length) for i in range(length)])]
    gather x2 -> x0, local copies, waits for them, and re-layouts: 3.55 us -> none  [the longest x1 2.81 us: per_device(): quad_values = placed.reshape(-1, restriction.shape[0])[elem_block]]
    scatter x3 -> x0, local copies, waits for them, and re-layouts: 3.06 us -> none  [the longest x1 1.17 us: per_device(): placed = jnp.zeros((tile_dev, row_width), jnp.float32).at[arrivals.reshap...]
    scatter x1 -> x0, other arithmetic: 2.12 us -> none  [per_device(): averaged = quad_values.at[shared_own].set(mixed)]
    all_to_all x3 -> x0, local copies, waits for them, and re-layouts: 1.7 us -> none  [the longest x2 1.19 us: per_device(): lax.all_to_all(where_to, 'ep', split_axis=0, concat_axis=0, tiled=True)]
  transfers between devices with their start and end apart: 3 -> 0, of which waited for: 3 -> 0; matrix products, arithmetic and copies ran while one was open for 9% -> 0% of each run, Pallas kernels for 0% -> 0%
where the time goes in v1:
time: 13.4 us; the launch traced here: 13.2 us
  Pallas kernels  11.9 us (89%)
  local copies, waits for them, and re-layouts  1.38 us (10%)
    pallas_call x1, Pallas kernels, per_device(): pl.pallas_call(functools.partial(kernel, n, cap), out_shape=jax.ShapeDtyp...  11.9 us
    unnamed x1, local copies, waits for them, and re-layouts  1.38 us

profile of v1, /device:TPU:0, one launch (start us, length us, event | category | flops | bytes accessed | tf_op | source)
XLA Modules:
  0.0 13.2 jit_solution(15237803516049663830)
XLA Ops:
  0.0 11.9 %shard_map.64 = f32[8,1024]{1,0:T(8,128)} custom-call(f32[128,512]{1,0:T(8,128)} %tension.1, s32[1,128]{1,0:T(1,128)} %bitcast.7, f32[8,64]{1,0:T(8,128)} %restriction.1, s32[8,128]{1,0:T(8,128)} %bitcast.4, s32[2,128]{1,0:T(2,128)} %bitcast.5, s32[2,128]{1,0:T(2,128)} %bitcast.6), custom_call_target="tpu_custom_call" | custom-call | tf_op jit(solution)/shard_map/pallas_call | solution.py:184
  11.9 1.4 %copy.8 = f32[8,1024]{1,0:T(8,128)} copy(f32[8,1024]{1,0:T(8,128)} %shard_map.64) | data formatting | bytes 65536

commit v2 on v1

--- a/solution.py
+++ b/solution.py
@@ -19,26 +19,36 @@
 
 def pieces(x):
     high = x.astype(BF16)
-    rest = x - high.astype(F32)
-    mid = rest.astype(BF16)
-    low = (rest - mid.astype(F32)).astype(BF16)
-    return jnp.concatenate([high, mid, low], axis=1)
+    return high, (x - high.astype(F32)).astype(BF16)
 
 
 def select_rows(onehot, x):
     lanes = x.shape[1]
-    got = jnp.dot(onehot, pieces(x), preferred_element_type=F32)
-    return got[:, :lanes] + got[:, lanes : 2 * lanes] + got[:, 2 * lanes :]
+    got = jnp.dot(onehot, jnp.concatenate(pieces(x), axis=1), preferred_element_type=F32)
+    return got[:, :lanes] + got[:, lanes:]
 
 
 def lanes_of(x, index):
     return jnp.take_along_axis(x, index, axis=1, mode="promise_in_bounds")
 
 
+def partner(me, k, n):
+    if True:
+        return lax.rem(me + k, n)
+    bit, peer = 1, 0
+    while bit < n:
+        have = lax.rem(me // bit, 2)
+        peer = peer + bit * (1 - have if k & bit else have)
+        bit *= 2
+    return peer
+
+
 def kernel(
-    n, cap, tension, dest, restriction, block, own, send, out,
-    outbox, inbox, ghost_out, ghost_in, send_sem, recv_sem, ghost_sem,
+    n, cap, *refs
 ):
+    given, out, held = refs[:6], refs[6], refs[7:13]
+    outbox, inbox, ghost_out, ghost_in, load_sem, send_sem, recv_sem, ghost_sem = refs[13:]
+    dest, send, block, restriction, own, tension = held
     me = lax.axis_index("ep")
     tiles = tension.shape[0]
     quad, nodes = restriction.shape
@@ -50,8 +60,14 @@
 
     barrier = pltpu.get_barrier_semaphore()
     for k in range(1, n):
-        pl.semaphore_signal(barrier, inc=1, device_id={"ep": lax.rem(me + k, n)})
-
+        pl.semaphore_signal(barrier, inc=1, device_id={"ep": partner(me, n - k, n)})
+
+    arrive = [pltpu.make_async_copy(a, b, load_sem.at[i]) for i, (a, b) in enumerate(zip(given, held))]
+    for copy in arrive:
+        copy.start()
+
+    arrive[1].wait()
+    arrive[2].wait()
     for h in range(halves):
         want = jnp.broadcast_to(send[h : h + 1, :], (rows_e, tiles))
         got = lanes_of(block[...], lax.rem(want, tiles))
@@ -60,6 +76,7 @@
             axis=0, keepdims=True,
         )
 
+    arrive[0].wait()
     place = dest[...]
     target = lax.div(place, tiles)
     to_peer = jnp.broadcast_to(target, (n, tiles)) == iota((n, tiles), 0)
@@ -77,14 +94,16 @@
     )
 
     full = (lanes, tension.shape[1])
+    arrive[3].wait()
     weight = jnp.concatenate([restriction[...]] * (full[1] // nodes), axis=1)
     weight = jnp.concatenate([weight] * (lanes // quad), axis=0)
     mine = lax.div(lax.rem(iota(full, 0), width), quad) == lax.div(iota(full, 1), nodes)
     weight = jnp.where(mine, weight, 0.0)
-    local = lax.dot_general(
-        tension[...], weight, MINOR,
-        precision=lax.Precision.HIGHEST, preferred_element_type=F32,
-    )
+    arrive[5].wait()
+    nodal, nodal_low = pieces(tension[...])
+    weight, weight_low = pieces(weight)
+    by = functools.partial(lax.dot_general, dimension_numbers=MINOR, preferred_element_type=F32)
+    local = by(nodal, weight) + (by(nodal_low, weight) + by(nodal, weight_low))
     packed = select_rows(pack, local)
     first = iota((cap, lanes), 1) < width
     for p in range(n):
@@ -98,7 +117,7 @@
     pl.semaphore_wait(barrier, n - 1)
     copies = []
     for k in range(1, n):
-        peer = lax.rem(me + k, n)
+        peer = partner(me, k, n)
         copies.append(
             pltpu.make_async_remote_copy(
                 src_ref=outbox.at[peer],
@@ -120,6 +139,7 @@
         copy.start()
     inbox[me] = outbox[me]
 
+    arrive[4].wait()
     owned = jnp.concatenate([own[h : h + 1, :] for h in range(halves)], axis=1)
     entry = (iota((rows_e, wide), 1) + 1).astype(F32)
     entry = jnp.where(
@@ -180,30 +200,34 @@
     quad, nodes = restriction.shape
     lanes = 2 * (tension.shape[1] // nodes * quad)
     halves = shared_own.shape[0] // tiles
-    vmem = pl.BlockSpec(memory_space=pltpu.VMEM)
+    given = (
+        tile_dest.reshape(1, tiles),
+        shared_send.reshape(halves, tiles),
+        elem_block.reshape(-1, tiles),
+        restriction,
+        shared_own.reshape(halves, tiles),
+        tension,
+    )
     return pl.pallas_call(
         functools.partial(kernel, n, cap),
         out_shape=jax.ShapeDtypeStruct((quad, elem_block.shape[0]), F32),
-        in_specs=[vmem] * 6,
-        out_specs=vmem,
-        scratch_shapes=[
+        in_specs=[pl.BlockSpec(memory_space=pltpu.HBM)] * 6,
+        out_specs=pl.BlockSpec(memory_space=pltpu.VMEM),
+        scratch_shapes=[pltpu.VMEM(a.shape, a.dtype) for a in given]
+        + [
             pltpu.VMEM((n, cap + 2, lanes), F32),
             pltpu.VMEM((n, cap + 2, lanes), F32),
             pltpu.VMEM((halves, tiles), I32),
             pltpu.VMEM((halves, tiles), I32),
+            pltpu.SemaphoreType.DMA((6,)),
             pltpu.SemaphoreType.DMA((n,)),
             pltpu.SemaphoreType.DMA((n,)),
             pltpu.SemaphoreType.DMA((2,)),
         ],
-        compiler_params=pltpu.CompilerParams(collective_id=0, has_side_effects=True),
-    )(
-        tension,
-        tile_dest.reshape(1, tiles),
-        restriction,
-        elem_block.reshape(-1, tiles),
-        shared_own.reshape(halves, tiles),
-        shared_send.reshape(halves, tiles),
-    )
+        compiler_params=pltpu.CompilerParams(
+            collective_id=0, has_side_effects=True, vmem_limit_bytes=60 * 1024 * 1024
+        ),
+    )(*given)
 
 
 def solution(mesh):

time: 13.4 us -> 12.7 us (0.948)
  Pallas kernels: 11.9 us -> 11.1 us
    pallas_call x1, Pallas kernels: 11.9 us -> 11.1 us  [per_device(): pl.pallas_call(functools.partial(kernel, n, cap), out_shape=jax.ShapeDtyp...]
where the time goes in v2:
time: 12.7 us; the launch traced here: 12.5 us
  Pallas kernels  11.1 us (87%)
  local copies, waits for them, and re-layouts  1.38 us (11%)
    pallas_call x1, Pallas kernels, per_device(): pl.pallas_call(functools.partial(kernel, n, cap), out_shape=jax.ShapeDtyp...  11.1 us
    unnamed x1, local copies, waits for them, and re-layouts  1.38 us

profile of v2, /device:TPU:0, one launch (start us, length us, event | category | flops | bytes accessed | tf_op | source)
XLA Modules:
  0.0 12.5 jit_solution(16444624360884815403)
XLA Ops:
  0.0 11.1 %shard_map.64 = f32[8,1024]{1,0:T(8,128)} custom-call(s32[1,128]{1,0:T(1,128)} %bitcast.7, s32[2,128]{1,0:T(2,128)} %bitcast.5, s32[8,128]{1,0:T(8,128)} %bitcast.4, f32[8,64]{1,0:T(8,128)} %refs_3_.1, s32[2,128]{1,0:T(2,128)} %bitcast.6, f32[128,512]{1,0:T(8,128)} %refs_5_.1), custom_call_target="tpu_custom_call" | custom-call | tf_op jit(solution)/shard_map/pallas_call | solution.py:211
  11.1 1.4 %copy.8 = f32[8,1024]{1,0:T(8,128)} copy(f32[8,1024]{1,0:T(8,128)} %shard_map.64) | data formatting | bytes 65536

commit v3 on v2

--- a/solution.py
+++ b/solution.py
@@ -63,20 +63,12 @@
         pl.semaphore_signal(barrier, inc=1, device_id={"ep": partner(me, n - k, n)})
 
     arrive = [pltpu.make_async_copy(a, b, load_sem.at[i]) for i, (a, b) in enumerate(zip(given, held))]
-    for copy in arrive:
-        copy.start()
-
-    arrive[1].wait()
-    arrive[2].wait()
-    for h in range(halves):
-        want = jnp.broadcast_to(send[h : h + 1, :], (rows_e, tiles))
-        got = lanes_of(block[...], lax.rem(want, tiles))
-        ghost_out[h : h + 1, :] = jnp.sum(
-            jnp.where(lax.div(want, tiles) == iota((rows_e, tiles), 0), got, 0),
-            axis=0, keepdims=True,
-        )
+    for i in (5, 0, 3, 1, 2, 4):
+        arrive[i].start()
 
     arrive[0].wait()
+    arrive[3].wait()
+    arrive[5].wait()
     place = dest[...]
     target = lax.div(place, tiles)
     to_peer = jnp.broadcast_to(target, (n, tiles)) == iota((n, tiles), 0)
@@ -94,12 +86,10 @@
     )
 
     full = (lanes, tension.shape[1])
-    arrive[3].wait()
     weight = jnp.concatenate([restriction[...]] * (full[1] // nodes), axis=1)
     weight = jnp.concatenate([weight] * (lanes // quad), axis=0)
     mine = lax.div(lax.rem(iota(full, 0), width), quad) == lax.div(iota(full, 1), nodes)
     weight = jnp.where(mine, weight, 0.0)
-    arrive[5].wait()
     nodal, nodal_low = pieces(tension[...])
     weight, weight_low = pieces(weight)
     by = functools.partial(lax.dot_general, dimension_numbers=MINOR, preferred_element_type=F32)
@@ -127,6 +117,17 @@
                 device_id={"ep": peer},
             )
         )
+    for copy in copies:
+        copy.start()
+    arrive[1].wait()
+    arrive[2].wait()
+    for h in range(halves):
+        want = jnp.broadcast_to(send[h : h + 1, :], (rows_e, tiles))
+        got = lanes_of(block[...], lax.rem(want, tiles))
+        ghost_out[h : h + 1, :] = jnp.sum(
+            jnp.where(lax.div(want, tiles) == iota((rows_e, tiles), 0), got, 0),
+            axis=0, keepdims=True,
+        )
     ghosts = pltpu.make_async_remote_copy(
         src_ref=ghost_out,
         dst_ref=ghost_in,
@@ -135,8 +136,6 @@
         device_id={"ep": lax.rem(me + n - 1, n)},
     )
     ghosts.start()
-    for copy in copies:
-        copy.start()
     inbox[me] = outbox[me]
 
     arrive[4].wait()
@@ -225,9 +224,9 @@
             pltpu.SemaphoreType.DMA((2,)),
         ],
         compiler_params=pltpu.CompilerParams(
-            collective_id=0, has_side_effects=True, vmem_limit_bytes=60 * 1024 * 1024
+            collective_id=0, has_side_effects=True, vmem_limit_bytes=16 * 2**20
         ),
-    )(*given)
+    )(*[pltpu.with_memory_space_constraint(a, pltpu.HBM) for a in given])
 
 
 def solution(mesh):

time: 12.7 us -> 11.1 us (0.87)
  Pallas kernels: 11.1 us -> 10.3 us
  local copies, waits for them, and re-layouts: 1.38 us -> 0.62 us
    pallas_call x1, Pallas kernels: 11.1 us -> 10.3 us  [per_device(): pl.pallas_call(functools.partial(kernel, n, cap), out_shape=jax.ShapeDtyp...]
    unnamed x1, local copies, waits for them, and re-layouts: 1.38 us -> 0.62 us
where the time goes in v3:
time: 11.1 us; the launch traced here: 11 us
  Pallas kernels  10.3 us (93%)
  local copies, waits for them, and re-layouts  0.62 us (6%)
    pallas_call x1, Pallas kernels, per_device(): pl.pallas_call(functools.partial(kernel, n, cap), out_shape=jax.ShapeDtyp...  10.3 us
    unnamed x1, local copies, waits for them, and re-layouts  0.62 us

profile of v3, /device:TPU:0, one launch (start us, length us, event | category | flops | bytes accessed | tf_op | source)
XLA Modules:
  0.0 11.0 jit_solution(6744447633307045749)
XLA Ops:
  0.0 10.3 %shard_map.64 = f32[8,1024]{1,0:T(8,128)S(1)} custom-call(s32[1,128]{1,0:T(1,128)} %bitcast.7, s32[2,128]{1,0:T(2,128)} %bitcast.5, s32[8,128]{1,0:T(8,128)} %bitcast.4, f32[8,64]{1,0:T(8,128)} %refs_3_.1, s32[2,128]{1,0:T(2,128)} %bitcast.6, f32[128,512]{1,0:T(8,128)} %refs_5_.1), custom_call_target="tpu_custom_call" | custom-call | tf_op jit(solution)/shard_map/pallas_call | solution.py:210
  10.3 0.6 %copy.8 = f32[8,1024]{1,0:T(8,128)} copy(f32[8,1024]{1,0:T(8,128)S(1)} %shard_map.64) | data formatting | bytes 65536

commit v4 on v3

--- a/solution.py
+++ b/solution.py
@@ -149,7 +149,13 @@
         entry, column.astype(F32).astype(BF16), MINOR, preferred_element_type=F32
     ).astype(I32)
 
+    blocks = width // quad
+    own_tile, own_part = lax.div(block[...], blocks), lax.rem(block[...], blocks)
+    number = jnp.maximum(shared - 1, 0)
+    ghost_half, ghost_lane = lax.div(number, tiles), lax.rem(number, tiles)
+
     ghosts.wait()
+    ghost_tile, ghost_part = lax.div(ghost_in[...], blocks), lax.rem(ghost_in[...], blocks)
     for copy in copies:
         copy.wait()
 
@@ -169,27 +175,25 @@
     placed = select_rows(jnp.concatenate(onehot, axis=0), arrived)
     placed = jnp.where(iota((tiles, lanes), 1) < width, placed[:tiles], placed[tiles:]).T
 
-    def values(index, base):
-        index = jnp.broadcast_to(index, (quad, tiles))
-        blocks = width // quad
-        tile, part = lax.div(index, blocks), lax.rem(index, blocks)
+    def spread(x, row):
+        return jnp.broadcast_to(x[row : row + 1, :], (quad, tiles))
+
+    def values(tile, part, base):
         got = lanes_of(placed[base : base + quad], tile)
         for b in range(1, blocks):
             low = base + b * quad
             got = jnp.where(part == b, lanes_of(placed[low : low + quad], tile), got)
         return got
 
-    ghost = [values(ghost_in[h : h + 1, :], width) for h in range(halves)]
+    ghost = [values(spread(ghost_tile, h), spread(ghost_part, h), width) for h in range(halves)]
     for r in range(rows_e):
-        mine = values(block[r : r + 1, :], 0)
-        which = jnp.broadcast_to(shared[r : r + 1, :], (quad, tiles))
-        number = jnp.maximum(which - 1, 0)
-        other = lanes_of(ghost[0], lax.rem(number, tiles))
+        mine = values(spread(own_tile, r), spread(own_part, r), 0)
+        other = lanes_of(ghost[0], spread(ghost_lane, r))
         for h in range(1, halves):
-            other = jnp.where(
-                lax.div(number, tiles) == h, lanes_of(ghost[h], lax.rem(number, tiles)), other
-            )
-        out[:, r * tiles : (r + 1) * tiles] = jnp.where(which > 0, 0.5 * (mine + other), mine)
+            other = jnp.where(spread(ghost_half, r) == h, lanes_of(ghost[h], spread(ghost_lane, r)), other)
+        out[:, r * tiles : (r + 1) * tiles] = jnp.where(
+            spread(shared, r) > 0, 0.5 * (mine + other), mine
+        )
 
 
 def per_device(tension, tile_dest, restriction, elem_block, shared_own, shared_send):

time: 11.1 us -> 11.1 us (level)
  no operation moved by 1% of the time
where the time goes in v4:
time: 11.1 us; the launch traced here: 11 us
  Pallas kernels  10.3 us (93%)
  local copies, waits for them, and re-layouts  0.62 us (6%)
    pallas_call x1, Pallas kernels, per_device(): pl.pallas_call(functools.partial(kernel, n, cap), out_shape=jax.ShapeDtyp...  10.3 us
    unnamed x1, local copies, waits for them, and re-layouts  0.62 us

profile of v4, /device:TPU:0, one launch (start us, length us, event | category | flops | bytes accessed | tf_op | source)
XLA Modules:
  0.0 11.0 jit_solution(12031284767729421310)
XLA Ops:
  0.0 10.3 %shard_map.64 = f32[8,1024]{1,0:T(8,128)S(1)} custom-call(s32[1,128]{1,0:T(1,128)} %bitcast.7, s32[2,128]{1,0:T(2,128)} %bitcast.5, s32[8,128]{1,0:T(8,128)} %bitcast.4, f32[8,64]{1,0:T(8,128)} %refs_3_.1, s32[2,128]{1,0:T(2,128)} %bitcast.6, f32[128,512]{1,0:T(8,128)} %refs_5_.1), custom_call_target="tpu_custom_call" | custom-call | tf_op jit(solution)/shard_map/pallas_call | solution.py:214
  10.3 0.6 %copy.8 = f32[8,1024]{1,0:T(8,128)} copy(f32[8,1024]{1,0:T(8,128)S(1)} %shard_map.64) | data formatting | bytes 65536
